TPU v7x, 32 devices: a whole 2x2x4 slice. The times are simulated.
32 devices in a mesh: vocab: 8 (over z, x), tok: 4 (over y, core).
Axes of the slice: x: 2, y: 2, z: 4, core: 2. Of those that a mesh axis runs over, the one named last changes fastest.
Arguments:
- hidden: bfloat16 [768, 7168], P('tok', 'vocab'), may hold values from -21 to 21
- head_weight: bfloat16 [7168, 8192], P('tok', 'vocab'), may hold values from -0.12695312 to 0.12695312
- targets: int32 [768], P('tok'), may hold values from 0 to 6143
- vocab_mask: int32 [8192], P('vocab'), may hold values from 0 to 1, as said below
- token_grad: float32 [768], P('tok'), may hold values from 16 to 160
Outputs:
- hidden_grad: bfloat16 [768, 7168], P('tok', 'vocab')
- token_loss: float32 [768], P('tok')
Inputs may be any that keep to these rules, and one draw needn't show every extreme that they name: vocab_mask is 1 on the columns below some cut and 0 from it on, with between 1 and 2048 zeros.
All inputs are finite; a program needn't handle non-finite values.
Results may differ from a plain program's by a relative error of at most 0.0051.
Values may be sent and summed in bfloat16 or wider, within the bound.
A program may use at most 64 MiB of HBM per device.

v0:
```python
import jax
import jax.numpy as jnp
from jax import lax
from jax.sharding import PartitionSpec as P


def combined_all(value, axis, join):
    pieces = jax.tree.map(lambda part: lax.all_gather(part, axis), value)
    head = jax.tree.map(lambda part: part[0], pieces)
    tail = jax.tree.map(lambda part: part[1:], pieces)
    running, _ = lax.scan(lambda running, share: (join(running, share), None), head, tail)
    return running


def combine_pairs(left_part, right_part):
    larger = jnp.maximum(left_part[0], right_part[0])
    summed = left_part[1] * jnp.exp(left_part[0] - larger) + right_part[1] * jnp.exp(
        right_part[0] - larger
    )
    return (larger, summed, left_part[2] + right_part[2])


def on_device(hidden, head_weight, targets, vocab_mask, token_grad):
    gathered = lax.all_gather(hidden, "vocab", axis=1, tiled=True)
    block_width = head_weight.shape[1]
    first_column = lax.axis_index("vocab") * block_width
    logits = jnp.dot(
        gathered,
        lax.all_gather(head_weight, "tok", axis=0, tiled=True),
        preferred_element_type=jnp.float32,
    )
    live_mask = vocab_mask[None, :] == 1
    masked = jnp.where(live_mask, logits, jnp.float32(-1e30))
    local_max = jnp.max(masked, axis=1)
    columns = first_column + jnp.arange(block_width, dtype=jnp.int32)
    onehot = columns[None, :] == targets[:, None]
    local_target = jnp.sum(jnp.where(onehot, logits, jnp.float32(0.0)), axis=1)
    local_sum = jnp.sum(jnp.exp(masked - local_max[:, None]), axis=1)
    row_max, denominator, target_logit = combined_all(
        (local_max, local_sum, local_target), "vocab", combine_pairs
    )
    log_norm = row_max + jnp.log(denominator)
    token_loss = log_norm - target_logit
    probabilities = jnp.exp(masked - log_norm[:, None])
    logit_grad = (token_grad[:, None] * (probabilities - onehot.astype(jnp.float32))).astype(
        jnp.bfloat16
    )
    partial_value = lax.dot_general(
        logit_grad,
        lax.all_gather(head_weight, "tok", axis=0, tiled=True),
        (((1,), (1,)), ((), ())),
        preferred_element_type=jnp.float32,
    )
    hidden_grad = lax.psum_scatter(partial_value, "vocab", scatter_dimension=1, tiled=True).astype(
        jnp.bfloat16
    )
    return (hidden_grad, token_loss)


def solution(mesh):
    placed = (P("tok", "vocab"), P("tok", "vocab"), P("tok"), P("vocab"), P("tok"))
    return jax.shard_map(
        on_device,
        mesh=mesh,
        in_specs=placed,
        out_specs=(P("tok", "vocab"), P("tok")),
        check_vma=False,
    )
```

profile of v0, /device:TPU:0, one launch (start us, length us, event | category | flops | bytes accessed | tf_op | source)
XLA Modules:
  0.0 334.8 jit_solution(9599591068299161233)
XLA Ops:
  7.2 0.0 all-gather.6.cloned.1.call-start
  7.2 0.7 all-gather.6.cloned.1.call-update
  7.9 0.0 all-gather.8.cloned.1.call-start
  7.9 0.7 all-gather.8.cloned.1.call-update
  8.6 0.0 copy-start
  8.7 0.0 reduce-scatter.2.cloned.1.call-start
  8.7 1.2 dynamic-slice
  10.6 0.7 broadcast_compare_fusion
  11.3 0.0 copy-start.1
  11.3 57.9 %all-gather.6.cloned.1.call-done = bf16[192,7168]{1,0:T(8,128)(2,1)} async-done(((bf16[192,896]{1,0:T(8,128)(2,1)}), bf16[192,7168]{1,0:T(8,128)(2,1)}) %all-gather.6.cloned.1.call-update) | async-done | bytes 2752528 | tf_op jit(solution)/shard_map/all_gather | solution.py:24
  69.2 93.7 %all-gather.8.cloned.1.call-done = bf16[7168,1024]{1,0:T(8,128)(2,1)} async-done(((bf16[1792,1024]{1,0:T(8,128)(2,1)}), bf16[7168,1024]{1,0:T(8,128)(2,1)}) %all-gather.8.cloned.1.call-update) | async-done | bytes 14680080 | tf_op jit(solution)/shard_map/all_gather | solution.py:29
  162.9 7.7 %select_reduce_fusion = (f32[192]{0:T(256)S(1)}, f32[192,1024]{1,0:T(8,128)S(1)}) fusion(pred[1024]{0:T(1024)(128)(4,1)S(1)} %broadcast_compare_fusion, bf16[192,7168]{1,0:T(8,128)(2,1)} %all-gather.6.cloned.1.call-done, bf16[7168,1024]{1,0:T(8,128)(2,1)} %all-gather.8.cloned.1.call-done), kind=kOutput, calls=%fused_computation.11 | convolution fusion | flops 2818965248 | bytes 18220800 | tf_op jit(solution)/shard_map/dot_general | solution.py:27
  170.6 0.3 dynamic-update-slice
  170.9 0.0 copy-done
  170.9 0.4 fusion
  171.3 0.3 dynamic-update-slice.1
  171.6 0.3 dynamic-update-slice.2
  171.8 37.0 %all-reduce.3 = (f32[1536]{0:T(1024)S(1)}, f32[1536]{0:T(1024)S(1)}, f32[1536]{0:T(1024)S(1)}) all-reduce(f32[1536]{0:T(1024)S(1)} %dynamic-update-slice, f32[1536]{0:T(1024)S(1)} %dynamic-update-slice.1, f32[1536]{0:T(1024)S(1)} %dynamic-update-slice.2), channel_id=2, replica_groups=mesh['vocab'=8,'tok'=4] {'vocab'}, use_global_device_ids=true, to_apply=%add | all-reduce | flops 4608 | bytes 36864
  208.8 0.1 slice.33
  208.9 0.1 slice.34
  209.0 0.1 slice.35
  209.0 0.1 reshape.23
  209.1 0.1 reshape.24
  209.2 0.1 reshape.25
  209.3 0.6 while.14
  209.8 0.6 fusion.13
  210.4 0.0 copy-done.1
  210.4 12.6 %fusion.4 = f32[192,7168]{1,0:T(8,128)} fusion(bf16[7168,1024]{1,0:T(8,128)(2,1)} %all-gather.8.cloned.1.call-done, f32[192,1024]{1,0:T(8,128)S(1)} %get-tuple-element.70, f32[192]{0:T(256)S(1)} %get-tuple-element.66, s32[1024]{0:T(1024)S(1)} %iota_add_fusion, f32[192]{0:T(256)S(1)} %copy-done.1, s32[192]{0:T(256)S(1)} %copy-done, ...), kind=kOutput, calls=%fused_computation.12 | convolution fusion | flops 2819948544 | bytes 20978944 | tf_op jit(solution)/shard_map/dot_general | solution.py:48
  223.0 0.0 reduce-scatter.2.cloned.1.call-update
  223.0 103.4 %reduce-scatter.2.cloned.1.call-done = f32[192,896]{1,0:T(8,128)} async-done(((f32[192,7168]{1,0:T(8,128)}), f32[192,896]{1,0:T(8,128)}) %reduce-scatter.2.cloned.1.call-update) | async-done | bytes 688144 | tf_op jit(solution)/shard_map/reduce_scatter | solution.py:54
  326.4 1.9 convert_element_type.11
  (35 shorter events, 0.4 us)
Async XLA Ops:
  7.2 62.1 %all-gather.6.cloned.1.call-start = ((), (), s32[]{:S(2)}) async-start(), calls=%async_computation.1 | async-start | bytes 3096576 | tf_op jit(solution)/shard_map/all_gather | solution.py:24
  7.9 155.1 %all-gather.8.cloned.1.call-start = ((), (), s32[]{:S(2)}) async-start(), calls=%async_computation.2 | async-start | bytes 18350080 | tf_op jit(solution)/shard_map/all_gather | solution.py:29
  8.6 162.3 %copy-start = (s32[192]{0:T(256)S(1)}, s32[192]{0:T(256)}, u32[]{:S(2)}) copy-start(s32[192]{0:T(256)} %param.9) | copy-start | bytes 2308
  8.7 317.8 %reduce-scatter.2.cloned.1.call-start = ((), (), s32[]{:S(2)}) async-start(), calls=%async_computation.3 | async-start | bytes 6193152 | tf_op jit(solution)/shard_map/reduce_scatter | solution.py:54
  11.3 199.1 %copy-start.1 = (f32[192]{0:T(256)S(1)}, f32[192]{0:T(256)}, u32[]{:S(2)}) copy-start(f32[192]{0:T(256)} %param.11) | copy-start | bytes 2308
Sparse Core Ops, SparseCore 0:
  10.1 59.0 all-gather.5
  70.8 92.1 all-gather.7
  223.1 103.2 reduce-scatter.1
where the time goes:
time: 335 us
  waiting for transfers between devices  256 us (76%)
  blocking collectives  37 us (11%)
  matrix products  20.3 us (6%)
  between operations  14.5 us (4%)
  other arithmetic  3.74 us (1%)
    reduce_scatter x1, waiting for transfers between devices, on_device(): lax.psum_scatter(partial_value, 'vocab', scatter_dimension=1, tiled=True)  103 us
    all_gather x1, waiting for transfers between devices, on_device(): lax.all_gather(head_weight, 'tok', axis=0, tiled=True)  93.7 us
    all_gather x1, waiting for transfers between devices, on_device(): gathered = lax.all_gather(hidden, 'vocab', axis=1, tiled=True)  57.9 us
    unnamed x1, blocking collectives  37 us
    dot_general x1, matrix products, on_device(): lax.dot_general(logit_grad, lax.all_gather(head_weight, 'tok', axis=0, ti...  12.6 us
    dot_general x1, matrix products, on_device(): jnp.dot(gathered, lax.all_gather(head_weight, 'tok', axis=0, tiled=True),...  7.66 us
  transfers between devices with their start and end apart: 3, of which 3 were waited for; matrix products, arithmetic and copies ran while one was open for 1% of the time, Pallas kernels for 0%

commit v1 on v0

--- a/solution.py
+++ b/solution.py
@@ -21,7 +21,13 @@
 
 
 def on_device(hidden, head_weight, targets, vocab_mask, token_grad):
-    gathered = lax.all_gather(hidden, "vocab", axis=1, tiled=True)
+    n_dev = lax.axis_size("vocab")
+    current, shards = (hidden, [hidden])
+    for _ in range(n_dev - 1):
+        current = lax.ppermute(current, "vocab", [(i, (i + 1) % n_dev) for i in range(n_dev)])
+        shards.insert(0, current)
+    row_of_blocks = jnp.concatenate(shards, axis=1)
+    gathered = jnp.roll(row_of_blocks, (lax.axis_index("vocab") + 1) * hidden.shape[1], axis=1)
     block_width = head_weight.shape[1]
     first_column = lax.axis_index("vocab") * block_width
     logits = jnp.dot(

time: 335 us -> 279 us (0.83)
  waiting for transfers between devices: 256 us -> 184 us
  local copies, waits for them, and re-layouts: 2.65 us -> 15.2 us
    all_gather x1, waiting for transfers between devices: 93.7 us -> 8.11 us  [on_device(): lax.all_gather(head_weight, 'tok', axis=0, tiled=True)]
    ppermute x0 -> x7, waiting for transfers between devices: none -> 72 us  [on_device(): lax.ppermute(current, 'vocab', [(i, (i + 1) % n_dev) for i in range(n_dev)])]
    all_gather x1 -> x0, waiting for transfers between devices: 57.9 us -> none  [on_device(): gathered = lax.all_gather(hidden, 'vocab', axis=1, tiled=True)]
    unnamed x11 -> x28, local copies, waits for them, and re-layouts: 2.07 us -> 13.8 us
  transfers between devices with their start and end apart: 3 -> 9, of which waited for: 3 -> 9; matrix products, arithmetic and copies ran while one was open for 1% -> 5% of each run, Pallas kernels for 0% -> 0%
where the time goes in v1:
time: 279 us
  waiting for transfers between devices  184 us (66%)
  blocking collectives  37 us (13%)
  matrix products  20.3 us (7%)
  local copies, waits for them, and re-layouts  15.2 us (5%)
  between operations  14.8 us (5%)
  other arithmetic  3.73 us (1%)
  starting transfers between devices  3.11 us (1%)
    reduce_scatter x1, waiting for transfers between devices, on_device(): lax.psum_scatter(partial_value, 'vocab', scatter_dimension=1, tiled=True)  103 us
    ppermute x7, waiting for transfers between devices, on_device(): lax.ppermute(current, 'vocab', [(i, (i + 1) % n_dev) for i in range(n_dev)])  72 us
    unnamed x1, blocking collectives  37 us
    unnamed x28, local copies, waits for them, and re-layouts  13.8 us
    dot_general x1, matrix products, on_device(): lax.dot_general(logit_grad, lax.all_gather(head_weight, 'tok', axis=0, ti...  12.6 us
    all_gather x1, waiting for transfers between devices, on_device(): lax.all_gather(head_weight, 'tok', axis=0, tiled=True)  8.11 us
    dot_general x1, matrix products, on_device(): jnp.dot(gathered, lax.all_gather(head_weight, 'tok', axis=0, tiled=True),...  7.72 us
  transfers between devices with their start and end apart: 9, of which 9 were waited for; matrix products, arithmetic and copies ran while one was open for 5% of the time, Pallas kernels for 0%

profile of v1, /device:TPU:0, one launch (start us, length us, event | category | flops | bytes accessed | tf_op | source)
XLA Modules:
  0.0 278.5 jit_solution(2367670656066571214)
XLA Ops:
  8.0 3.0 %collective-permute-start = (bf16[192,896]{1,0:T(8,128)(2,1)}, bf16[192,896]{1,0:T(8,128)(2,1)S(1)}, u32[]{:S(2)}, u32[]{:S(2)}) collective-permute-start(bf16[192,896]{1,0:T(8,128)(2,1)} %param.7), channel_id=1, source_target_pairs={{0,4},{4,8},{8,12},{12,16},{16,20},{20,24},{24,28},{28,0},{1,5},{5... | collective-permute-start | bytes 1032200 | tf_op jit(solution)/shard_map/ppermute | solution.py:27
  11.0 11.3 %collective-permute-done = bf16[192,896]{1,0:T(8,128)(2,1)S(1)} collective-permute-done((bf16[192,896]{1,0:T(8,128)(2,1)}, bf16[192,896]{1,0:T(8,128)(2,1)S(1)}, u32[]{:S(2)}, u32[]{:S(2)}) %collective-permute-start) | collective-permute-done | bytes 344096 | tf_op jit(solution)/shard_map/ppermute | solution.py:27
  22.3 11.9 %collective-permute-done.1 = bf16[192,896]{1,0:T(8,128)(2,1)S(1)} collective-permute-done((bf16[192,896]{1,0:T(8,128)(2,1)S(1)}, bf16[192,896]{1,0:T(8,128)(2,1)S(1)}, u32[]{:S(2)}, u32[]{:S(2)}) %collective-permute-start.1) | collective-permute-done | bytes 344096 | tf_op jit(solution)/shard_map/ppermute | solution.py:27
  34.2 11.1 %collective-permute-done.2 = bf16[192,896]{1,0:T(8,128)(2,1)S(1)} collective-permute-done((bf16[192,896]{1,0:T(8,128)(2,1)S(1)}, bf16[192,896]{1,0:T(8,128)(2,1)S(1)}, u32[]{:S(2)}, u32[]{:S(2)}) %collective-permute-start.2) | collective-permute-done | bytes 344096 | tf_op jit(solution)/shard_map/ppermute | solution.py:27
  45.3 10.2 %collective-permute-done.3 = bf16[192,896]{1,0:T(8,128)(2,1)S(1)} collective-permute-done((bf16[192,896]{1,0:T(8,128)(2,1)S(1)}, bf16[192,896]{1,0:T(8,128)(2,1)S(1)}, u32[]{:S(2)}, u32[]{:S(2)}) %collective-permute-start.3) | collective-permute-done | bytes 344096 | tf_op jit(solution)/shard_map/ppermute | solution.py:27
  55.5 9.9 %collective-permute-done.4 = bf16[192,896]{1,0:T(8,128)(2,1)S(1)} collective-permute-done((bf16[192,896]{1,0:T(8,128)(2,1)S(1)}, bf16[192,896]{1,0:T(8,128)(2,1)S(1)}, u32[]{:S(2)}, u32[]{:S(2)}) %collective-permute-start.4) | collective-permute-done | bytes 344096 | tf_op jit(solution)/shard_map/ppermute | solution.py:27
  65.4 10.3 %collective-permute-done.5 = bf16[192,896]{1,0:T(8,128)(2,1)S(1)} collective-permute-done((bf16[192,896]{1,0:T(8,128)(2,1)S(1)}, bf16[192,896]{1,0:T(8,128)(2,1)S(1)}, u32[]{:S(2)}, u32[]{:S(2)}) %collective-permute-start.5) | collective-permute-done | bytes 344096 | tf_op jit(solution)/shard_map/ppermute | solution.py:27
  75.7 1.2 dynamic-slice
  77.6 0.7 broadcast_compare_fusion
  78.3 7.3 %collective-permute-done.6 = bf16[192,896]{1,0:T(8,128)(2,1)S(1)} collective-permute-done((bf16[192,896]{1,0:T(8,128)(2,1)S(1)}, bf16[192,896]{1,0:T(8,128)(2,1)S(1)}, u32[]{:S(2)}, u32[]{:S(2)}) %collective-permute-start.6) | collective-permute-done | bytes 344096 | tf_op jit(solution)/shard_map/ppermute | solution.py:27
  85.6 0.8 constant_dynamic-update-slice_fusion.15
  86.4 0.8 constant_dynamic-update-slice_fusion.14
  87.2 0.8 constant_dynamic-update-slice_fusion.13
  88.0 0.8 constant_dynamic-update-slice_fusion.12
  88.8 0.8 constant_dynamic-update-slice_fusion.11
  89.6 0.8 constant_dynamic-update-slice_fusion.10
  90.4 0.8 constant_dynamic-update-slice_fusion.9
  91.1 0.8 constant_dynamic-update-slice_fusion.8
  91.9 0.8 constant_dynamic-update-slice_fusion.7
  92.7 0.8 constant_dynamic-update-slice_fusion.6
  93.5 0.8 constant_dynamic-update-slice_fusion.5
  94.3 0.8 constant_dynamic-update-slice_fusion.4
  95.0 0.8 constant_dynamic-update-slice_fusion.3
  95.8 0.8 constant_dynamic-update-slice_fusion.2
  96.6 0.8 constant_dynamic-update-slice_fusion.1
  97.4 0.8 constant_dynamic-update-slice_fusion
  98.2 8.1 %all-gather.5.cloned.1.call-done = bf16[7168,1024]{1,0:T(8,128)(2,1)} async-done(((bf16[1792,1024]{1,0:T(8,128)(2,1)}), bf16[7168,1024]{1,0:T(8,128)(2,1)}) %all-gather.5.cloned.1.call-update) | async-done | bytes 14680080 | tf_op jit(solution)/shard_map/all_gather | solution.py:35
  106.3 7.7 %select_reduce_fusion = (f32[192]{0:T(256)S(1)}, f32[192,1024]{1,0:T(8,128)S(1)}) fusion(pred[1024]{0:T(1024)(128)(4,1)S(1)} %broadcast_compare_fusion, bf16[7168,1024]{1,0:T(8,128)(2,1)} %all-gather.5.cloned.1.call-done, bf16[192,14336]{1,0:T(8,128)(2,1)} %constant_dynamic-update-slice_fusion, s32[]{:T(128)S(6)} %select_n.22), kind=kOutput, calls=%fused_computation.13 | convolution fusion | flops 2818965248 | bytes 18220804 | tf_op jit(solution)/shard_map/dot_general | solution.py:33
  115.2 37.0 %all-reduce.3 = (f32[1536]{0:T(1024)S(1)}, f32[1536]{0:T(1024)S(1)}, f32[1536]{0:T(1024)S(1)}) all-reduce(f32[1536]{0:T(1024)S(1)} %dynamic-update-slice, f32[1536]{0:T(1024)S(1)} %dynamic-update-slice.1, f32[1536]{0:T(1024)S(1)} %dynamic-update-slice.2), channel_id=2, replica_groups=mesh['vocab'=8,'tok'=4] {'vocab'}, use_global_device_ids=true, to_apply=%add | all-reduce | flops 4608 | bytes 36864
  153.8 12.6 %fusion.6 = f32[192,7168]{1,0:T(8,128)} fusion(bf16[7168,1024]{1,0:T(8,128)(2,1)} %all-gather.5.cloned.1.call-done, f32[192,1024]{1,0:T(8,128)S(1)} %get-tuple-element.70, f32[192]{0:T(256)S(1)} %get-tuple-element.66, s32[1024]{0:T(1024)S(1)} %iota_add_fusion, f32[192]{0:T(256)S(1)} %copy-done.2, s32[192]{0:T(256)S(1)} %copy-done.1, ...), kind=kOutput, calls=%fused_computation.14 | convolution fusion | flops 2819948544 | bytes 20978944 | tf_op jit(solution)/shard_map/dot_general | solution.py:54
  166.4 103.4 %reduce-scatter.2.cloned.1.call-done = f32[192,896]{1,0:T(8,128)} async-done(((f32[192,7168]{1,0:T(8,128)}), f32[192,896]{1,0:T(8,128)}) %reduce-scatter.2.cloned.1.call-update) | async-done | bytes 688144 | tf_op jit(solution)/shard_map/reduce_scatter | solution.py:60
  269.8 1.9 convert_element_type.11
  (63 shorter events, 3.9 us)
Async XLA Ops:
  7.2 84.0 %copy-start = (bf16[192,896]{1,0:T(8,128)(2,1)S(1)}, bf16[192,896]{1,0:T(8,128)(2,1)}, u32[]{:S(2)}) copy-start(bf16[192,896]{1,0:T(8,128)(2,1)} %param.7) | copy-start | bytes 1032196
  7.2 99.1 %all-gather.5.cloned.1.call-start = ((), (), s32[]{:S(2)}) async-start(), calls=%async_computation.1 | async-start | bytes 18350080 | tf_op jit(solution)/shard_map/all_gather | solution.py:35
  7.9 261.9 %reduce-scatter.2.cloned.1.call-start = ((), (), s32[]{:S(2)}) async-start(), calls=%async_computation.2 | async-start | bytes 6193152 | tf_op jit(solution)/shard_map/reduce_scatter | solution.py:60
  8.0 14.3 %collective-permute-start = (bf16[192,896]{1,0:T(8,128)(2,1)}, bf16[192,896]{1,0:T(8,128)(2,1)S(1)}, u32[]{:S(2)}, u32[]{:S(2)}) collective-permute-start(bf16[192,896]{1,0:T(8,128)(2,1)} %param.7), channel_id=1, source_target_pairs={{0,4},{4,8},{8,12},{12,16},{16,20},{20,24},{24,28},{28,0},{1,5},{5... | collective-permute-start | bytes 1032200 | tf_op jit(solution)/shard_map/ppermute | solution.py:27
  22.3 11.9 %collective-permute-start.1 = (bf16[192,896]{1,0:T(8,128)(2,1)S(1)}, bf16[192,896]{1,0:T(8,128)(2,1)S(1)}, u32[]{:S(2)}, u32[]{:S(2)}) collective-permute-start(bf16[192,896]{1,0:T(8,128)(2,1)S(1)} %collective-permute-done), channel_id=1, source_target_pairs={{0,4},{4,8},{8,12},{12,16},{16,20},{20,24},{24,28},{28,0},{1,5},{5... | collective-permute-start | bytes 1032200 | tf_op jit(solution)/shard_map/ppermute | solution.py:27
  34.2 11.1 %collective-permute-start.2 = (bf16[192,896]{1,0:T(8,128)(2,1)S(1)}, bf16[192,896]{1,0:T(8,128)(2,1)S(1)}, u32[]{:S(2)}, u32[]{:S(2)}) collective-permute-start(bf16[192,896]{1,0:T(8,128)(2,1)S(1)} %collective-permute-done.1), channel_id=1, source_target_pairs={{0,4},{4,8},{8,12},{12,16},{16,20},{20,24},{24,28},{28,0},{1,5},{5... | collective-permute-start | bytes 1032200 | tf_op jit(solution)/shard_map/ppermute | solution.py:27
  45.3 10.2 %collective-permute-start.3 = (bf16[192,896]{1,0:T(8,128)(2,1)S(1)}, bf16[192,896]{1,0:T(8,128)(2,1)S(1)}, u32[]{:S(2)}, u32[]{:S(2)}) collective-permute-start(bf16[192,896]{1,0:T(8,128)(2,1)S(1)} %collective-permute-done.2), channel_id=1, source_target_pairs={{0,4},{4,8},{8,12},{12,16},{16,20},{20,24},{24,28},{28,0},{1,5},{5... | collective-permute-start | bytes 1032200 | tf_op jit(solution)/shard_map/ppermute | solution.py:27
  55.5 9.9 %collective-permute-start.4 = (bf16[192,896]{1,0:T(8,128)(2,1)S(1)}, bf16[192,896]{1,0:T(8,128)(2,1)S(1)}, u32[]{:S(2)}, u32[]{:S(2)}) collective-permute-start(bf16[192,896]{1,0:T(8,128)(2,1)S(1)} %collective-permute-done.3), channel_id=1, source_target_pairs={{0,4},{4,8},{8,12},{12,16},{16,20},{20,24},{24,28},{28,0},{1,5},{5... | collective-permute-start | bytes 1032200 | tf_op jit(solution)/shard_map/ppermute | solution.py:27
  65.4 10.3 %collective-permute-start.5 = (bf16[192,896]{1,0:T(8,128)(2,1)S(1)}, bf16[192,896]{1,0:T(8,128)(2,1)S(1)}, u32[]{:S(2)}, u32[]{:S(2)}) collective-permute-start(bf16[192,896]{1,0:T(8,128)(2,1)S(1)} %collective-permute-done.4), channel_id=1, source_target_pairs={{0,4},{4,8},{8,12},{12,16},{16,20},{20,24},{24,28},{28,0},{1,5},{5... | collective-permute-start | bytes 1032200 | tf_op jit(solution)/shard_map/ppermute | solution.py:27
  75.7 9.9 %collective-permute-start.6 = (bf16[192,896]{1,0:T(8,128)(2,1)S(1)}, bf16[192,896]{1,0:T(8,128)(2,1)S(1)}, u32[]{:S(2)}, u32[]{:S(2)}) collective-permute-start(bf16[192,896]{1,0:T(8,128)(2,1)S(1)} %collective-permute-done.5), channel_id=1, source_target_pairs={{0,4},{4,8},{8,12},{12,16},{16,20},{20,24},{24,28},{28,0},{1,5},{5... | collective-permute-start | bytes 1032200 | tf_op jit(solution)/shard_map/ppermute | solution.py:27
  98.2 16.1 %copy-start.1 = (s32[192]{0:T(256)S(1)}, s32[192]{0:T(256)}, u32[]{:S(2)}) copy-start(s32[192]{0:T(256)} %param.9) | copy-start | bytes 2308
  98.2 55.6 %copy-start.2 = (f32[192]{0:T(256)S(1)}, f32[192]{0:T(256)}, u32[]{:S(2)}) copy-start(f32[192]{0:T(256)} %param.11) | copy-start | bytes 2308
Sparse Core Ops, SparseCore 0:
  9.5 96.7 all-gather.4
  166.5 103.2 reduce-scatter.1
